TPU v7x, 32 devices: a whole 2x2x4 slice. The times are simulated.
32 devices in a mesh: grp: 2 (over x), row: 16 (over z, y, core).
Axes of the slice: x: 2, y: 2, z: 4, core: 2. Of those that a mesh axis runs over, the one named last changes fastest.
Arguments:
- alignment: bfloat16 [128, 128, 256], P(('grp', 'row')), parts along dimension 0, may hold values from -6 to 6
- seq_flags: int32 [128], P(('grp', 'row')), parts along dimension 0, may hold values 0 or 1
- crop_flags: int32 [256], P('grp'), parts along dimension 0, may hold values 0 or 1
- norm_gain: float32 [256], replicated, may hold values from 0.5 to 1.5
- norm_bias: float32 [256], replicated, may hold values from -3 to 3
- left_weight: bfloat16 [256, 32], replicated, may hold values from -0.375 to 0.375
- left_bias: float32 [32], replicated, may hold values from -3 to 3
- right_weight: bfloat16 [256, 32], replicated, may hold values from -0.375 to 0.375
- right_bias: float32 [32], replicated, may hold values from -3 to 3
- out_weight: bfloat16 [1024, 128], replicated, may hold values from -0.1875 to 0.1875
- out_bias: float32 [128], replicated, may hold values from -3 to 3
Outputs:
- pair_update: bfloat16 [256, 128, 128], P(('grp', 'row')), parts along dimension 0
There are 2 independent parts, one for each index of `grp`. A program takes and returns all parts, laid end to end along the dimension named above; an argument that names none is the same for every part. Nothing has to cross between parts.
All inputs are finite; a program needn't handle non-finite values. No bound on the sum of `seq_flags` on one device may be relied on, other than what follows from the above.
Results may differ from a plain program's by a relative error of at most 0.004.
Values may be sent and summed in bfloat16 or wider, within the bound.
No kernel may reach another device: no remote copies, remote signals or barrier semaphores. Data moves between devices by JAX's collectives and lax.ppermute only.
A program may use at most 128 MiB of HBM per device.

v0:
```python
import jax
import jax.numpy as jnp
from jax import lax
from jax.sharding import PartitionSpec as P


def normalize(values, norm_gain, norm_bias):
    values = values.astype(jnp.float32)
    average = jnp.mean(values, axis=-1, keepdims=True)
    variance = jnp.mean((values - average) ** 2, axis=-1, keepdims=True)
    return (values - average) * lax.rsqrt(variance + 1e-05) * norm_gain + norm_bias


def project(normed, weight, bias, scaling):
    product = jnp.einsum(
        "src,cd->srd", normed, weight.astype(jnp.float32), precision=lax.Precision.HIGHEST
    )
    return ((product + bias) * scaling).astype(jnp.bfloat16)


def pair_tile(
    left_flat, column_piece, crop_rows, crop_cols, live_count, out_weight, out_bias, channels
):
    rows_here = crop_rows.shape[0]
    width_cols = column_piece.shape[1] // channels
    sums = lax.dot_general(
        left_flat, column_piece, (((0,), (0,)), ((), ())), preferred_element_type=jnp.float32
    )
    outer_sum = sums.reshape(rows_here, channels, width_cols, channels).transpose(0, 2, 1, 3)
    outer_sum = outer_sum.reshape(rows_here * width_cols, channels * channels).astype(jnp.bfloat16)
    projected = jnp.dot(outer_sum, out_weight, preferred_element_type=jnp.float32)
    projected = projected.reshape(rows_here, width_cols, out_weight.shape[1])
    divisor = jnp.maximum(live_count * crop_rows[:, None] * crop_cols[None, :], 1.0)
    return (projected / divisor[:, :, None] + out_bias).astype(jnp.bfloat16)


def column_blocks(
    left_flat, column_piece, crop_rows, crop_cols, live_count, out_weight, out_bias, channels
):
    rows_here = crop_rows.shape[0]
    width_cols = column_piece.shape[1] // channels
    span = max(1, 2048 // rows_here)
    if width_cols > span and width_cols % span == 0:

        def one_block(block_index):
            start = block_index * span
            piece_block = lax.dynamic_slice_in_dim(
                column_piece, start * channels, span * channels, 1
            )
            crop_block = lax.dynamic_slice_in_dim(crop_cols, start, span, 0)
            return pair_tile(
                left_flat,
                piece_block,
                crop_rows,
                crop_block,
                live_count,
                out_weight,
                out_bias,
                channels,
            )

        stacked = lax.map(one_block, jnp.arange(width_cols // span, dtype=jnp.int32))
        return stacked.transpose(1, 0, 2, 3).reshape(rows_here, width_cols, out_weight.shape[1])
    return pair_tile(
        left_flat, column_piece, crop_rows, crop_cols, live_count, out_weight, out_bias, channels
    )


def per_device(
    alignment,
    seq_flags,
    crop_flags,
    norm_gain,
    norm_bias,
    left_weight,
    left_bias,
    right_weight,
    right_bias,
    out_weight,
    out_bias,
):
    channels = left_weight.shape[1]
    devices_row = lax.axis_size("row")
    residues = alignment.shape[1]
    rows_here = residues // devices_row
    crop_float = crop_flags.astype(jnp.float32)
    my_index = lax.axis_index("row")
    crop_rows = lax.dynamic_slice_in_dim(crop_float, my_index * rows_here, rows_here, 0)
    regrouped = lax.all_to_all(alignment, "row", split_axis=1, concat_axis=0, tiled=True)
    all_flags = lax.all_gather(seq_flags, "row", axis=0, tiled=True)
    flag_float = all_flags.astype(jnp.float32)
    live_count = jnp.sum(flag_float)
    normed = normalize(regrouped, norm_gain, norm_bias)
    scaling = flag_float[:, None, None] * crop_rows[None, :, None]
    left = project(normed, left_weight, left_bias, scaling)
    right = project(normed, right_weight, right_bias, scaling)
    sequences = left.shape[0]
    left_flat = left.reshape(sequences, rows_here * channels)
    right_flat = right.reshape(sequences, rows_here * channels)
    return column_blocks(
        left_flat,
        lax.all_gather(right_flat, "row", axis=1, tiled=True),
        crop_rows,
        crop_float,
        live_count,
        out_weight,
        out_bias,
        channels,
    )


def solution(mesh):
    return jax.shard_map(
        per_device,
        mesh=mesh,
        in_specs=(
            P(("grp", "row"), None, None),
            P(("grp", "row")),
            P("grp"),
            P(),
            P(),
            P(),
            P(),
            P(),
            P(),
            P(),
            P(),
        ),
        out_specs=P(("grp", "row"), None, None),
        check_vma=False,
    )
```

profile of v0, /device:TPU:0, one launch (start us, length us, event | category | flops | bytes accessed | tf_op | source)
XLA Modules:
  0.0 54.4 jit_solution(9916558976857848131)
XLA Ops:
  0.0 1.9 %copy.75 = bf16[4,128,256]{2,0,1:T(4,128)(2,1)} copy(bf16[4,128,256]{2,1,0:T(8,128)(2,1)} %param.11) | data formatting | bytes 524288 | tf_op args[0]
  1.9 7.4 %all-to-all-start = ((bf16[4,128,256]{2,0,1:T(4,128)(2,1)}), bf16[4,128,256]{2,0,1:T(4,128)(2,1)S(1)}, u32[]{:S(2)}, u32[]{:S(2)}) async-start(bf16[4,128,256]{2,0,1:T(4,128)(2,1)} %copy.75), calls=%async_computation | async-start | bytes 524288 | tf_op jit(solution)/shard_map/all_to_all | solution.py:89
  9.4 1.3 %dynamic-slice = u32[1]{0:T(128)} dynamic-slice(u32[32]{0:T(128)} %constant.24, u32[]{:T(128)S(6)} %add.58), dynamic_slice_sizes={1} | dynamic-slice | bytes 12
  11.4 0.9 %dynamic-update-slice = s32[64]{0:T(128)S(1)} dynamic-update-slice(s32[64]{0:T(128)S(1)} %broadcast.80, s32[4]{0:T(128)} %param.12, u32[]{:T(128)} %bitcast.7) | dynamic-update-slice | bytes 36
  12.2 12.4 %all-reduce = s32[64]{0:T(128)S(1)} all-reduce(s32[64]{0:T(128)S(1)} %dynamic-update-slice), channel_id=1, replica_groups=mesh['grp'=2,'row'=16] {'row'}, use_global_device_ids=true, to_apply=%add | all-reduce | flops 64 | bytes 512
  24.7 0.7 %convert_reduce_fusion = f32[]{:T(128)} fusion(s32[64]{0:T(128)S(1)} %all-reduce), kind=kLoop, calls=%fused_computation.27 | loop fusion | flops 127 | bytes 260 | tf_op jit(solution)/shard_map/reduce_sum | solution.py:92
  25.4 0.7 %convert_element_type.51 = f32[128]{0:T(128)S(1)} convert(s32[128]{0:T(128)} %param.13) | non-fusion elementwise | flops 128 | bytes 1024 | tf_op jit(solution)/shard_map/convert_element_type | solution.py:86
  26.0 0.8 %broadcast_multiply_fusion.2 = (f32[8]{0:T(128)S(1)}, f32[8]{0:T(128)S(1)}) fusion(f32[]{:T(128)} %convert_reduce_fusion, f32[128]{0:T(128)S(1)} %convert_element_type.51, s32[]{:T(128)S(6)} %select_n.3), kind=kLoop, calls=%fused_computation.26 | loop fusion | flops 8 | bytes 104 | tf_op jit(solution)/shard_map/mul | solution.py:33
  26.8 0.1 multiply_maximum_fusion
  26.9 0.1 fusion.10
  27.2 0.1 copy.81
  27.2 0.1 copy.80
  27.3 0.3 multiply_reduce_fusion
  27.7 0.1 copy.84
  27.9 0.2 fusion.9
  28.2 0.4 fusion.5
  28.5 0.1 copy.86
  28.7 21.0 %all_gather.7 = bf16[64,4096]{0,1:T(8,128)(2,1)S(1)} all-gather(bf16[64,256]{0,1:T(8,128)(2,1)S(1)} %bitcast.57), channel_id=1, replica_groups=mesh['grp'=2,'row'=16] {'row'}, dimensions={1}, use_global_device_ids=true | all-gather | bytes 557056 | tf_op jit(solution)/shard_map/all_gather | solution.py:102
  49.7 1.1 %copy.87 = bf16[128,32,64]{0,2,1:T(8,128)(2,1)S(1)} copy(bf16[128,32,64]{2,1,0:T(8,128)(2,1)S(1)} %bitcast.55) | data formatting | bytes 1048576 | tf_op jit(solution)/shard_map/dot_general | solution.py:26
  50.8 0.4 fusion.4
  51.2 0.1 copy.85
  51.3 0.7 %convert_bitcast_fusion = bf16[8,128,32,32]{1,2,3,0:T(8,128)(2,1)S(1)} fusion(bf16[128,32,64]{0,2,1:T(8,128)(2,1)S(1)} %copy.87, bf16[64,8,32]{0,2,1:T(8,128)(2,1)S(1)} %copy.85), kind=kOutput, calls=%fused_computation | convolution fusion | flops 135266304 | bytes 2654208 | tf_op jit(solution)/shard_map/dot_general | solution.py:26
  52.0 0.8 %copy.88 = bf16[8,128,32,32]{1,3,2,0:T(8,128)(2,1)S(1)} copy(bf16[8,128,32,32]{1,2,3,0:T(8,128)(2,1)S(1)} %convert_bitcast_fusion) | data formatting | bytes 4194304 | tf_op jit(solution)/shard_map/convert_element_type | solution.py:30
  52.9 1.5 %fusion.1 = bf16[8,128,128]{2,1,0:T(8,128)(2,1)} fusion(bf16[8,128,1024]{1,2,0:T(8,128)(2,1)S(1)} %bitcast.56, bf16[1024,128]{1,0:T(8,128)(2,1)S(1)} %copy-done, f32[128]{0:T(128)S(1)} %copy-done.7, f32[8,128]{1,0:T(8,128)S(1)} %multiply_maximum_fusion), kind=kOutput, calls=%fused_computation.3 | convolution fusion | flops 268828672 | bytes 2626048 | tf_op jit(solution)/shard_map/dot_general | solution.py:31
  (26 shorter events, 0.4 us)
Async XLA Ops:
  0.0 52.9 %copy-start = (bf16[1024,128]{1,0:T(8,128)(2,1)S(1)}, bf16[1024,128]{1,0:T(8,128)(2,1)}, u32[]{:S(2)}) copy-start(bf16[1024,128]{1,0:T(8,128)(2,1)} %param.20) | copy-start | bytes 786436
  0.0 27.9 %copy-start.4 = (f32[256]{0:T(256)S(1)}, f32[256]{0:T(256)}, u32[]{:S(2)}) copy-start(f32[256]{0:T(256)} %param.14) | copy-start | bytes 3076
  0.0 27.9 %copy-start.3 = (f32[256]{0:T(256)S(1)}, f32[256]{0:T(256)}, u32[]{:S(2)}) copy-start(f32[256]{0:T(256)} %param.15) | copy-start | bytes 3076
  1.9 25.0 %all-to-all-start = ((bf16[4,128,256]{2,0,1:T(4,128)(2,1)}), bf16[4,128,256]{2,0,1:T(4,128)(2,1)S(1)}, u32[]{:S(2)}, u32[]{:S(2)}) async-start(bf16[4,128,256]{2,0,1:T(4,128)(2,1)} %copy.75), calls=%async_computation | async-start | bytes 524288 | tf_op jit(solution)/shard_map/all_to_all | solution.py:89
  9.3 18.8 %copy-start.1 = (bf16[256,32]{0,1:T(8,128)(2,1)S(1)}, bf16[256,32]{0,1:T(8,128)(2,1)}, u32[]{:S(2)}) copy-start(bf16[256,32]{0,1:T(8,128)(2,1)} %param.18) | copy-start | bytes 49156
  9.3 18.8 %copy-start.5 = (f32[32]{0:T(128)S(1)}, f32[32]{0:T(128)}, u32[]{:S(2)}) copy-start(f32[32]{0:T(128)} %param.19) | copy-start | bytes 388
  27.9 22.9 %copy-start.2 = (bf16[256,32]{0,1:T(8,128)(2,1)S(1)}, bf16[256,32]{0,1:T(8,128)(2,1)}, u32[]{:S(2)}) copy-start(bf16[256,32]{0,1:T(8,128)(2,1)} %param.16) | copy-start | bytes 49156
  27.9 22.9 %copy-start.6 = (f32[32]{0:T(128)S(1)}, f32[32]{0:T(128)}, u32[]{:S(2)}) copy-start(f32[32]{0:T(128)} %param.17) | copy-start | bytes 388
  52.0 0.8 %copy-start.7 = (f32[128]{0:T(128)S(1)}, f32[128]{0:T(128)}, u32[]{:S(2)}) copy-start(f32[128]{0:T(128)} %param.21) | copy-start | bytes 1540
where the time goes:
time: 54.7 us; the launch traced here: 54.4 us
  blocking collectives  33.5 us (61%)
  starting transfers between devices  7.42 us (14%)
  local copies, waits for them, and re-layouts  6.75 us (12%)
  other arithmetic  2.94 us (5%)
  matrix products  2.91 us (5%)
  between operations  0.9 us (2%)
    all_gather x1, blocking collectives, per_device(): lax.all_gather(right_flat, 'row', axis=1, tiled=True)  21 us
    unnamed x1, blocking collectives  12.4 us
    all_to_all x1, starting transfers between devices, per_device(): lax.all_to_all(alignment, 'row', split_axis=1, concat_axis=0, tiled=True)  7.42 us
    unnamed x20, local copies, waits for them, and re-layouts  4.12 us
    dot_general x1, matrix products, pair_tile(): jnp.dot(outer_sum, out_weight, preferred_element_type=jnp.float32)  1.49 us
    dot_general x1, local copies, waits for them, and re-layouts, pair_tile(): lax.dot_general(left_flat, column_piece, (((0,), (0,)), ((), ())), prefer...  1.11 us
  transfers between devices with their start and end apart: 1, of which 0 were waited for; matrix products, arithmetic and copies ran while one was open for 8% of the time, Pallas kernels for 0%

commit v1 on v0

--- a/solution.py
+++ b/solution.py
@@ -2,6 +2,18 @@
 import jax.numpy as jnp
 from jax import lax
 from jax.sharding import PartitionSpec as P
+
+
+def cut_along(x, dim, size):
+    dims = x.shape
+    parts = x.reshape(*dims[:dim], size, dims[dim] // size, *dims[dim + 1 :])
+    return jnp.moveaxis(parts, dim, 0)
+
+
+def in_order(blocks, dim):
+    blocks = jnp.moveaxis(blocks, 0, dim)
+    dims = blocks.shape
+    return blocks.reshape(*dims[:dim], dims[dim] * dims[dim + 1], *dims[dim + 2 :])
 
 
 def normalize(values, norm_gain, norm_bias):
@@ -86,7 +98,14 @@
     crop_float = crop_flags.astype(jnp.float32)
     my_index = lax.axis_index("row")
     crop_rows = lax.dynamic_slice_in_dim(crop_float, my_index * rows_here, rows_here, 0)
-    regrouped = lax.all_to_all(alignment, "row", split_axis=1, concat_axis=0, tiled=True)
+    size, index = (lax.axis_size("row"), lax.axis_index("row"))
+    blocks = cut_along(alignment, 1, size)
+    outs = [blocks[index]]
+    for step in range(1, size):
+        sent = blocks[(index + step) % size]
+        outs.append(lax.ppermute(sent, "row", [(i, (i + step) % size) for i in range(size)]))
+    blocks = jnp.stack(outs)[(index - jnp.arange(size)) % size]
+    regrouped = in_order(blocks, 0)
     all_flags = lax.all_gather(seq_flags, "row", axis=0, tiled=True)
     flag_float = all_flags.astype(jnp.float32)
     live_count = jnp.sum(flag_float)

time: 54.7 us -> 73.1 us (1.34)
  starting transfers between devices: 7.42 us -> 21.2 us
  blocking collectives: 33.5 us -> 36.8 us
  waiting for transfers between devices: 0.01 us -> 1.42 us
    ppermute x0 -> x15, starting transfers between devices: none -> 21.2 us  [per_device(): lax.ppermute(sent, 'row', [(i, (i + step) % size) for i in range(size)])]
    all_to_all x1 -> x0, starting transfers between devices: 7.42 us -> none  [per_device(): lax.all_to_all(alignment, 'row', split_axis=1, concat_axis=0, tiled=True)]
    all_gather x1, blocking collectives: 21 us -> 24.8 us  [per_device(): lax.all_gather(right_flat, 'row', axis=1, tiled=True)]
    ppermute x0 -> x15, waiting for transfers between devices: none -> 1.42 us  [per_device(): lax.ppermute(sent, 'row', [(i, (i + step) % size) for i in range(size)])]
    unnamed x20 -> x34, local copies, waits for them, and re-layouts: 4.12 us -> 2.89 us
    squeeze x0 -> x1, local copies, waits for them, and re-layouts: none -> 0.97 us  [per_device(): sent = blocks[(index + step) % size]]
  transfers between devices with their start and end apart: 1 -> 15, of which waited for: 0 -> 2; matrix products, arithmetic and copies ran while one was open for 8% -> 7% of each run, Pallas kernels for 0% -> 0%
where the time goes in v1:
time: 73.1 us; the launch traced here: 72.9 us
  blocking collectives  36.8 us (50%)
  starting transfers between devices  21.2 us (29%)
  local copies, waits for them, and re-layouts  6.63 us (9%)
  matrix products  2.91 us (4%)
  other arithmetic  2.83 us (4%)
  waiting for transfers between devices  1.42 us (2%)
  between operations  1.13 us (2%)
    all_gather x1, blocking collectives, per_device(): lax.all_gather(right_flat, 'row', axis=1, tiled=True)  24.8 us
    ppermute x15, starting transfers between devices, per_device(): lax.ppermute(sent, 'row', [(i, (i + step) % size) for i in range(size)])  21.2 us
    unnamed x1, blocking collectives  12 us
    unnamed x34, local copies, waits for them, and re-layouts  2.89 us
    dot_general x1, matrix products, pair_tile(): jnp.dot(outer_sum, out_weight, preferred_element_type=jnp.float32)  1.49 us
  transfers between devices with their start and end apart: 15, of which 2 were waited for; matrix products, arithmetic and copies ran while one was open for 7% of the time, Pallas kernels for 0%

profile of v1, /device:TPU:0, one launch (start us, length us, event | category | flops | bytes accessed | tf_op | source)
XLA Modules:
  0.0 72.9 jit_solution(7267451593020646863)
XLA Ops:
  0.2 1.0 %dynamic-slice_bitcast_fusion = (bf16[4,8,256]{2,1,0:T(8,128)(2,1)S(1)}, bf16[4,8,256]{2,1,0:T(8,128)(2,1)S(1)}, bf16[4,8,256]{2,1,0:T(8,128)(2,1)S(1)}, bf16[4,...) fusion(bf16[4,16,8,256]{3,2,1,0:T(8,128)(2,1)} %bitcast.113, ...), kind=kLoop, calls=%fused_computation.41 | loop fusion | bytes 491580 | tf_op jit(solution)/shard_map/squeeze | solution.py:105
  1.8 2.6 %collective-permute-start.1 = (bf16[4,8,256]{2,1,0:T(8,128)(2,1)S(1)}, bf16[4,8,256]{2,1,0:T(8,128)(2,1)S(1)}, u32[]{:S(2)}, u32[]{:S(2)}) collective-permute-start(bf16[4,8,256]{2,1,0:T(8,128)(2,1)S(1)} %get-tuple-element.20), channel_id=1, source_target_pairs={{0,2},{1,3},{2,4},{3,5},{4,6},{5,7},{6,8},{7,9},{8,10},{9,11},{10,... | collective-permute-start | bytes 49160 | tf_op jit(solution)/shard_map/ppermute | solution.py:106
  4.3 2.4 %collective-permute-start.2 = (bf16[4,8,256]{2,1,0:T(8,128)(2,1)S(1)}, bf16[4,8,256]{2,1,0:T(8,128)(2,1)S(1)}, u32[]{:S(2)}, u32[]{:S(2)}) collective-permute-start(bf16[4,8,256]{2,1,0:T(8,128)(2,1)S(1)} %get-tuple-element.19), channel_id=1, source_target_pairs={{0,3},{1,4},{2,5},{3,6},{4,7},{5,8},{6,9},{7,10},{8,11},{9,12},{10... | collective-permute-start | bytes 49160 | tf_op jit(solution)/shard_map/ppermute | solution.py:106
  6.7 1.6 %collective-permute-start.3 = (bf16[4,8,256]{2,1,0:T(8,128)(2,1)S(1)}, bf16[4,8,256]{2,1,0:T(8,128)(2,1)S(1)}, u32[]{:S(2)}, u32[]{:S(2)}) collective-permute-start(bf16[4,8,256]{2,1,0:T(8,128)(2,1)S(1)} %get-tuple-element.18), channel_id=1, source_target_pairs={{0,4},{1,5},{2,6},{3,7},{4,8},{5,9},{6,10},{7,11},{8,12},{9,13},{1... | collective-permute-start | bytes 49160 | tf_op jit(solution)/shard_map/ppermute | solution.py:106
  8.5 1.2 %dynamic-slice.64 = u32[1]{0:T(128)} dynamic-slice(u32[32]{0:T(128)} %constant.129, u32[]{:T(128)S(6)} %add.268), dynamic_slice_sizes={1} | dynamic-slice | bytes 12
  10.4 0.9 %dynamic-update-slice = s32[64]{0:T(128)S(1)} dynamic-update-slice(s32[64]{0:T(128)S(1)} %broadcast.159, s32[4]{0:T(128)} %param.12, u32[]{:T(128)} %bitcast.37) | dynamic-update-slice | bytes 36
  11.3 12.0 %all-reduce = s32[64]{0:T(128)S(1)} all-reduce(s32[64]{0:T(128)S(1)} %dynamic-update-slice), channel_id=1, replica_groups=mesh['grp'=2,'row'=16] {'row'}, use_global_device_ids=true, to_apply=%add | all-reduce | flops 64 | bytes 512
  23.3 0.6 convert_reduce_fusion.1
  23.9 0.7 constant_dynamic-update-slice_fusion.15
  24.6 0.7 convert_element_type.41
  25.3 0.7 broadcast_multiply_fusion.2
  26.2 1.4 %collective-permute-start.5 = (bf16[4,8,256]{2,1,0:T(8,128)(2,1)S(1)}, bf16[4,8,256]{2,1,0:T(8,128)(2,1)S(1)}, u32[]{:S(2)}, u32[]{:S(2)}) collective-permute-start(bf16[4,8,256]{2,1,0:T(8,128)(2,1)S(1)} %get-tuple-element.16), channel_id=1, source_target_pairs={{0,6},{1,7},{2,8},{3,9},{4,10},{5,11},{6,12},{7,13},{8,14},{9,15},... | collective-permute-start | bytes 49160 | tf_op jit(solution)/shard_map/ppermute | solution.py:106
  28.1 2.3 %collective-permute-start.8 = (bf16[4,8,256]{2,1,0:T(8,128)(2,1)S(1)}, bf16[4,8,256]{2,1,0:T(8,128)(2,1)S(1)}, u32[]{:S(2)}, u32[]{:S(2)}) collective-permute-start(bf16[4,8,256]{2,1,0:T(8,128)(2,1)S(1)} %get-tuple-element.13), channel_id=1, source_target_pairs={{0,9},{1,10},{2,11},{3,12},{4,13},{5,14},{6,15},{7,0},{8,1},{9,2},... | collective-permute-start | bytes 49160 | tf_op jit(solution)/shard_map/ppermute | solution.py:106
  30.4 3.3 %collective-permute-start.9 = (bf16[4,8,256]{2,1,0:T(8,128)(2,1)S(1)}, bf16[4,8,256]{2,1,0:T(8,128)(2,1)S(1)}, u32[]{:S(2)}, u32[]{:S(2)}) collective-permute-start(bf16[4,8,256]{2,1,0:T(8,128)(2,1)S(1)} %get-tuple-element.12), channel_id=1, source_target_pairs={{0,10},{1,11},{2,12},{3,13},{4,14},{5,15},{6,0},{7,1},{8,2},{9,3},... | collective-permute-start | bytes 49160 | tf_op jit(solution)/shard_map/ppermute | solution.py:106
  33.7 0.6 collective-permute-start.10
  34.3 1.8 %collective-permute-start.11 = (bf16[4,8,256]{2,1,0:T(8,128)(2,1)S(1)}, bf16[4,8,256]{2,1,0:T(8,128)(2,1)S(1)}, u32[]{:S(2)}, u32[]{:S(2)}) collective-permute-start(bf16[4,8,256]{2,1,0:T(8,128)(2,1)S(1)} %get-tuple-element.10), channel_id=1, source_target_pairs={{0,12},{1,13},{2,14},{3,15},{4,0},{5,1},{6,2},{7,3},{8,4},{9,5},{1... | collective-permute-start | bytes 49160 | tf_op jit(solution)/shard_map/ppermute | solution.py:106
  36.6 2.3 %collective-permute-start.13 = (bf16[4,8,256]{2,1,0:T(8,128)(2,1)S(1)}, bf16[4,8,256]{2,1,0:T(8,128)(2,1)S(1)}, u32[]{:S(2)}, u32[]{:S(2)}) collective-permute-start(bf16[4,8,256]{2,1,0:T(8,128)(2,1)S(1)} %get-tuple-element.8), channel_id=1, source_target_pairs={{0,14},{1,15},{2,0},{3,1},{4,2},{5,3},{6,4},{7,5},{8,6},{9,7},{10,... | collective-permute-start | bytes 49160 | tf_op jit(solution)/shard_map/ppermute | solution.py:106
  39.0 1.2 %collective-permute-start.14 = (bf16[4,8,256]{2,1,0:T(8,128)(2,1)S(1)}, bf16[4,8,256]{2,1,0:T(8,128)(2,1)S(1)}, u32[]{:S(2)}, u32[]{:S(2)}) collective-permute-start(bf16[4,8,256]{2,1,0:T(8,128)(2,1)S(1)} %get-tuple-element.7), channel_id=1, source_target_pairs={{0,15},{1,0},{2,1},{3,2},{4,3},{5,4},{6,5},{7,6},{8,7},{9,8},{10,9... | collective-permute-start | bytes 49160 | tf_op jit(solution)/shard_map/ppermute | solution.py:106
  40.4 1.2 %collective-permute-done.14 = bf16[4,8,256]{2,1,0:T(8,128)(2,1)S(1)} collective-permute-done((bf16[4,8,256]{2,1,0:T(8,128)(2,1)S(1)}, bf16[4,8,256]{2,1,0:T(8,128)(2,1)S(1)}, u32[]{:S(2)}, u32[]{:S(2)}) %collective-permute-start.14) | collective-permute-done | bytes 16416 | tf_op jit(solution)/shard_map/ppermute | solution.py:106
  43.5 24.8 %all_gather.7 = bf16[64,4096]{0,1:T(8,128)(2,1)S(1)} all-gather(bf16[64,256]{0,1:T(8,128)(2,1)S(1)} %bitcast.112), channel_id=1, replica_groups=mesh['grp'=2,'row'=16] {'row'}, dimensions={1}, use_global_device_ids=true | all-gather | bytes 557056 | tf_op jit(solution)/shard_map/all_gather | solution.py:121
  68.2 1.1 %copy.15 = bf16[128,32,64]{0,2,1:T(8,128)(2,1)S(1)} copy(bf16[128,32,64]{2,1,0:T(8,128)(2,1)S(1)} %bitcast.109) | data formatting | bytes 1048576 | tf_op jit(solution)/shard_map/dot_general | solution.py:38
  69.8 0.7 convert_bitcast_fusion
  70.5 0.8 %copy.16 = bf16[8,128,32,32]{1,3,2,0:T(8,128)(2,1)S(1)} copy(bf16[8,128,32,32]{1,2,3,0:T(8,128)(2,1)S(1)} %convert_bitcast_fusion) | data formatting | bytes 4194304 | tf_op jit(solution)/shard_map/convert_element_type | solution.py:42
  71.4 1.5 %fusion.1 = bf16[8,128,128]{2,1,0:T(8,128)(2,1)} fusion(bf16[8,128,1024]{1,2,0:T(8,128)(2,1)S(1)} %bitcast.110, bf16[1024,128]{1,0:T(8,128)(2,1)S(1)} %copy-done, f32[128]{0:T(128)S(1)} %copy-done.7, f32[8,128]{1,0:T(8,128)S(1)} %multiply_maximum_fusion), kind=kOutput, calls=%fused_computation.4 | convolution fusion | flops 268828672 | bytes 2626048 | tf_op jit(solution)/shard_map/dot_general | solution.py:43
  (66 shorter events, 4.5 us)
Async XLA Ops:
  0.0 71.4 %copy-start = (bf16[1024,128]{1,0:T(8,128)(2,1)S(1)}, bf16[1024,128]{1,0:T(8,128)(2,1)}, u32[]{:S(2)}) copy-start(bf16[1024,128]{1,0:T(8,128)(2,1)} %param.20) | copy-start | bytes 786436
  0.0 42.7 %copy-start.4 = (f32[256]{0:T(256)S(1)}, f32[256]{0:T(256)}, u32[]{:S(2)}) copy-start(f32[256]{0:T(256)} %param.14) | copy-start | bytes 3076
  0.0 42.7 %copy-start.3 = (f32[256]{0:T(256)S(1)}, f32[256]{0:T(256)}, u32[]{:S(2)}) copy-start(f32[256]{0:T(256)} %param.15) | copy-start | bytes 3076
  0.0 42.9 %copy-start.1 = (bf16[256,32]{0,1:T(8,128)(2,1)S(1)}, bf16[256,32]{0,1:T(8,128)(2,1)}, u32[]{:S(2)}) copy-start(bf16[256,32]{0,1:T(8,128)(2,1)} %param.18) | copy-start | bytes 49156
  0.0 42.9 %copy-start.5 = (f32[32]{0:T(128)S(1)}, f32[32]{0:T(128)}, u32[]{:S(2)}) copy-start(f32[32]{0:T(128)} %param.19) | copy-start | bytes 388
  1.2 25.0 %collective-permute-start = (bf16[4,8,256]{2,1,0:T(8,128)(2,1)S(1)}, bf16[4,8,256]{2,1,0:T(8,128)(2,1)S(1)}, u32[]{:S(2)}, u32[]{:S(2)}) collective-permute-start(bf16[4,8,256]{2,1,0:T(8,128)(2,1)S(1)} %get-tuple-element.21), channel_id=1, source_target_pairs={{0,1},{1,2},{2,3},{3,4},{4,5},{5,6},{6,7},{7,8},{8,9},{9,10},{10,1... | collective-permute-start | bytes 49160 | tf_op jit(solution)/shard_map/ppermute | solution.py:106
  1.8 25.8 %collective-permute-start.1 = (bf16[4,8,256]{2,1,0:T(8,128)(2,1)S(1)}, bf16[4,8,256]{2,1,0:T(8,128)(2,1)S(1)}, u32[]{:S(2)}, u32[]{:S(2)}) collective-permute-start(bf16[4,8,256]{2,1,0:T(8,128)(2,1)S(1)} %get-tuple-element.20), channel_id=1, source_target_pairs={{0,2},{1,3},{2,4},{3,5},{4,6},{5,7},{6,8},{7,9},{8,10},{9,11},{10,... | collective-permute-start | bytes 49160 | tf_op jit(solution)/shard_map/ppermute | solution.py:106
  4.3 23.2 %collective-permute-start.2 = (bf16[4,8,256]{2,1,0:T(8,128)(2,1)S(1)}, bf16[4,8,256]{2,1,0:T(8,128)(2,1)S(1)}, u32[]{:S(2)}, u32[]{:S(2)}) collective-permute-start(bf16[4,8,256]{2,1,0:T(8,128)(2,1)S(1)} %get-tuple-element.19), channel_id=1, source_target_pairs={{0,3},{1,4},{2,5},{3,6},{4,7},{5,8},{6,9},{7,10},{8,11},{9,12},{10... | collective-permute-start | bytes 49160 | tf_op jit(solution)/shard_map/ppermute | solution.py:106
  6.7 21.3 %collective-permute-start.3 = (bf16[4,8,256]{2,1,0:T(8,128)(2,1)S(1)}, bf16[4,8,256]{2,1,0:T(8,128)(2,1)S(1)}, u32[]{:S(2)}, u32[]{:S(2)}) collective-permute-start(bf16[4,8,256]{2,1,0:T(8,128)(2,1)S(1)} %get-tuple-element.18), channel_id=1, source_target_pairs={{0,4},{1,5},{2,6},{3,7},{4,8},{5,9},{6,10},{7,11},{8,12},{9,13},{1... | collective-permute-start | bytes 49160 | tf_op jit(solution)/shard_map/ppermute | solution.py:106
  8.3 22.0 %collective-permute-start.4 = (bf16[4,8,256]{2,1,0:T(8,128)(2,1)S(1)}, bf16[4,8,256]{2,1,0:T(8,128)(2,1)S(1)}, u32[]{:S(2)}, u32[]{:S(2)}) collective-permute-start(bf16[4,8,256]{2,1,0:T(8,128)(2,1)S(1)} %get-tuple-element.17), channel_id=1, source_target_pairs={{0,5},{1,6},{2,7},{3,8},{4,9},{5,10},{6,11},{7,12},{8,13},{9,14},{... | collective-permute-start | bytes 49160 | tf_op jit(solution)/shard_map/ppermute | solution.py:106
  26.2 7.5 %collective-permute-start.5 = (bf16[4,8,256]{2,1,0:T(8,128)(2,1)S(1)}, bf16[4,8,256]{2,1,0:T(8,128)(2,1)S(1)}, u32[]{:S(2)}, u32[]{:S(2)}) collective-permute-start(bf16[4,8,256]{2,1,0:T(8,128)(2,1)S(1)} %get-tuple-element.16), channel_id=1, source_target_pairs={{0,6},{1,7},{2,8},{3,9},{4,10},{5,11},{6,12},{7,13},{8,14},{9,15},... | collective-permute-start | bytes 49160 | tf_op jit(solution)/shard_map/ppermute | solution.py:106
  27.5 6.8 %collective-permute-start.6 = (bf16[4,8,256]{2,1,0:T(8,128)(2,1)S(1)}, bf16[4,8,256]{2,1,0:T(8,128)(2,1)S(1)}, u32[]{:S(2)}, u32[]{:S(2)}) collective-permute-start(bf16[4,8,256]{2,1,0:T(8,128)(2,1)S(1)} %get-tuple-element.15), channel_id=1, source_target_pairs={{0,7},{1,8},{2,9},{3,10},{4,11},{5,12},{6,13},{7,14},{8,15},{9,0},... | collective-permute-start | bytes 49160 | tf_op jit(solution)/shard_map/ppermute | solution.py:106
  27.5 8.6 %collective-permute-start.7 = (bf16[4,8,256]{2,1,0:T(8,128)(2,1)S(1)}, bf16[4,8,256]{2,1,0:T(8,128)(2,1)S(1)}, u32[]{:S(2)}, u32[]{:S(2)}) collective-permute-start(bf16[4,8,256]{2,1,0:T(8,128)(2,1)S(1)} %get-tuple-element.14), channel_id=1, source_target_pairs={{0,8},{1,9},{2,10},{3,11},{4,12},{5,13},{6,14},{7,15},{8,0},{9,1},... | collective-permute-start | bytes 49160 | tf_op jit(solution)/shard_map/ppermute | solution.py:106
  28.1 8.6 %collective-permute-start.8 = (bf16[4,8,256]{2,1,0:T(8,128)(2,1)S(1)}, bf16[4,8,256]{2,1,0:T(8,128)(2,1)S(1)}, u32[]{:S(2)}, u32[]{:S(2)}) collective-permute-start(bf16[4,8,256]{2,1,0:T(8,128)(2,1)S(1)} %get-tuple-element.13), channel_id=1, source_target_pairs={{0,9},{1,10},{2,11},{3,12},{4,13},{5,14},{6,15},{7,0},{8,1},{9,2},... | collective-permute-start | bytes 49160 | tf_op jit(solution)/shard_map/ppermute | solution.py:106
  30.4 8.6 %collective-permute-start.9 = (bf16[4,8,256]{2,1,0:T(8,128)(2,1)S(1)}, bf16[4,8,256]{2,1,0:T(8,128)(2,1)S(1)}, u32[]{:S(2)}, u32[]{:S(2)}) collective-permute-start(bf16[4,8,256]{2,1,0:T(8,128)(2,1)S(1)} %get-tuple-element.12), channel_id=1, source_target_pairs={{0,10},{1,11},{2,12},{3,13},{4,14},{5,15},{6,0},{7,1},{8,2},{9,3},... | collective-permute-start | bytes 49160 | tf_op jit(solution)/shard_map/ppermute | solution.py:106
  33.7 6.5 %collective-permute-start.10 = (bf16[4,8,256]{2,1,0:T(8,128)(2,1)S(1)}, bf16[4,8,256]{2,1,0:T(8,128)(2,1)S(1)}, u32[]{:S(2)}, u32[]{:S(2)}) collective-permute-start(bf16[4,8,256]{2,1,0:T(8,128)(2,1)S(1)} %get-tuple-element.11), channel_id=1, source_target_pairs={{0,11},{1,12},{2,13},{3,14},{4,15},{5,0},{6,1},{7,2},{8,3},{9,4},{... | collective-permute-start | bytes 49160 | tf_op jit(solution)/shard_map/ppermute | solution.py:106
  34.3 5.8 %collective-permute-start.11 = (bf16[4,8,256]{2,1,0:T(8,128)(2,1)S(1)}, bf16[4,8,256]{2,1,0:T(8,128)(2,1)S(1)}, u32[]{:S(2)}, u32[]{:S(2)}) collective-permute-start(bf16[4,8,256]{2,1,0:T(8,128)(2,1)S(1)} %get-tuple-element.10), channel_id=1, source_target_pairs={{0,12},{1,13},{2,14},{3,15},{4,0},{5,1},{6,2},{7,3},{8,4},{9,5},{1... | collective-permute-start | bytes 49160 | tf_op jit(solution)/shard_map/ppermute | solution.py:106
  36.1 4.0 %collective-permute-start.12 = (bf16[4,8,256]{2,1,0:T(8,128)(2,1)S(1)}, bf16[4,8,256]{2,1,0:T(8,128)(2,1)S(1)}, u32[]{:S(2)}, u32[]{:S(2)}) collective-permute-start(bf16[4,8,256]{2,1,0:T(8,128)(2,1)S(1)} %get-tuple-element.9), channel_id=1, source_target_pairs={{0,13},{1,14},{2,15},{3,0},{4,1},{5,2},{6,3},{7,4},{8,5},{9,6},{10... | collective-permute-start | bytes 49160 | tf_op jit(solution)/shard_map/ppermute | solution.py:106
  36.6 3.8 %collective-permute-start.13 = (bf16[4,8,256]{2,1,0:T(8,128)(2,1)S(1)}, bf16[4,8,256]{2,1,0:T(8,128)(2,1)S(1)}, u32[]{:S(2)}, u32[]{:S(2)}) collective-permute-start(bf16[4,8,256]{2,1,0:T(8,128)(2,1)S(1)} %get-tuple-element.8), channel_id=1, source_target_pairs={{0,14},{1,15},{2,0},{3,1},{4,2},{5,3},{6,4},{7,5},{8,6},{9,7},{10,... | collective-permute-start | bytes 49160 | tf_op jit(solution)/shard_map/ppermute | solution.py:106
  39.0 2.6 %collective-permute-start.14 = (bf16[4,8,256]{2,1,0:T(8,128)(2,1)S(1)}, bf16[4,8,256]{2,1,0:T(8,128)(2,1)S(1)}, u32[]{:S(2)}, u32[]{:S(2)}) collective-permute-start(bf16[4,8,256]{2,1,0:T(8,128)(2,1)S(1)} %get-tuple-element.7), channel_id=1, source_target_pairs={{0,15},{1,0},{2,1},{3,2},{4,3},{5,4},{6,5},{7,6},{8,7},{9,8},{10,9... | collective-permute-start | bytes 49160 | tf_op jit(solution)/shard_map/ppermute | solution.py:106
  42.7 26.6 %copy-start.2 = (bf16[256,32]{0,1:T(8,128)(2,1)S(1)}, bf16[256,32]{0,1:T(8,128)(2,1)}, u32[]{:S(2)}) copy-start(bf16[256,32]{0,1:T(8,128)(2,1)} %param.16) | copy-start | bytes 49156
  42.7 26.6 %copy-start.6 = (f32[32]{0:T(128)S(1)}, f32[32]{0:T(128)}, u32[]{:S(2)}) copy-start(f32[32]{0:T(128)} %param.17) | copy-start | bytes 388
  70.5 0.8 %copy-start.7 = (f32[128]{0:T(128)S(1)}, f32[128]{0:T(128)}, u32[]{:S(2)}) copy-start(f32[128]{0:T(128)} %param.21) | copy-start | bytes 1540
